TPU v7x, 512 devices: a whole 4x8x8 slice. The times are simulated.
512 devices in a mesh: seq: 128 (over z, y, core), tp: 4 (over x).
Axes of the slice: x: 4, y: 8, z: 8, core: 2. Of those that a mesh axis runs over, the one named last changes fastest.
Arguments:
- queries: bfloat16 [12288, 4096], P('seq', 'tp'), may hold values from -8 to 8
- keys: bfloat16 [12288, 1024], P('seq', 'tp'), may hold values from -7 to 7
- values: bfloat16 [12288, 1024], P('seq', 'tp'), may hold values from -24 to 24
- router_prob: float32 [12288], P('seq'), may hold values from 0.2 to 1
- norm_gain: float32 [4096], P('tp'), may hold values from 0.25 to 1.75
- slot_pos: int32 [12288], P('seq'), may hold values from 0 to 255, as said below
- live_count: int32 [128], P('seq'), may hold values from 1 to 96, 4096 in all
Outputs:
- routed: bfloat16 [32768, 4096], P('seq', 'tp')
Inputs may be any that keep to these rules, and one draw needn't show every extreme that they name: The slots of a shard that are live are its first live_count slots; the counts add up to 4096 and the largest is 96. Within each shard's 96 slots the positions are distinct and ascending; slot a of shard s stands for the token s * 256 + slot_pos[a].
All inputs are finite; a program needn't handle non-finite values.
Results may differ from a plain program's by a relative error of at most 0.007.
Values may be sent and summed in bfloat16 or wider, within the bound.
No kernel may reach another device: no remote copies, remote signals or barrier semaphores. Data moves between devices by JAX's collectives and lax.ppermute only.
A program may use at most 64 MiB of HBM per device.

v0:
```python
import math

import jax
import jax.numpy as jnp
from jax import lax
from jax.sharding import PartitionSpec as P

H = 32
HD = 128
TOK_DEV = 256


far_number = 1 << 30
epsilon = 1e-06
block_limit = 1024
lowest = -1e30


def in_one_piece(arrays, axis, split_dim, concat_dim, along):
    widths = [a.shape[along] for a in arrays]
    both = jnp.concatenate(arrays, axis=along)
    whole = lax.all_to_all(both, axis, split_axis=split_dim, concat_axis=concat_dim, tiled=True)
    return tuple(jnp.split(whole, [sum(widths[:k]) for k in range(1, len(widths))], axis=along))


def sent_together(arrays, axis, dim, along):
    ends, at = ([], 0)
    for a in arrays[:-1]:
        at += a.shape[along]
        ends.append(at)
    both = jnp.concatenate(arrays, axis=along)
    return tuple(jnp.split(lax.all_gather(both, axis, axis=dim, tiled=True), ends, axis=along))


def from_everyone(shard, axis):
    copies = jnp.broadcast_to(shard, (lax.axis_size(axis), *shard.shape))
    return lax.all_to_all(copies, axis, split_axis=0, concat_axis=0, tiled=True)


def taken_together(shard, axis):
    everything = from_everyone(shard, axis)
    return jnp.sum(everything, axis=0)


def attend_block(
    carried,
    current_key_block,
    value_block,
    key_numbers,
    head_grouped_rows,
    query_numbers,
    score_scale,
):
    highest, totals, running_output = carried
    scores = (
        jnp.einsum(
            "zpeo,jpo->pezj",
            head_grouped_rows,
            current_key_block,
            preferred_element_type=jnp.float32,
        )
        * score_scale
    )
    visible = key_numbers[None, None, None, :] <= query_numbers[None, None, :, None]
    masked = jnp.where(visible, scores, lowest)
    newest = jnp.maximum(highest, jnp.max(masked, axis=-1))
    weights = jnp.where(visible, jnp.exp(scores - newest[..., None]), 0.0)
    factor = jnp.exp(highest - newest)
    totals = totals * factor + jnp.sum(weights, axis=-1)
    update = jnp.einsum(
        "ycwh,hyu->ycwu",
        weights.astype(jnp.bfloat16),
        value_block,
        preferred_element_type=jnp.float32,
    )
    running_output = running_output * factor[..., None] + update
    return (newest, totals, running_output)


def fold_blocks(
    carried, key_all, value_all, head_grouped_rows, query_numbers, number_rule, score_scale
):
    length = key_all.shape[0]
    block_rows = min(length, block_limit)
    block_count = -(-length // block_rows)
    offsets = jnp.arange(block_count * block_rows, dtype=jnp.int32)
    numbers = jnp.where(offsets < length, number_rule(offsets), far_number)
    count_of_heads = key_all.shape[1] // HD
    key_blocks = key_all.reshape(block_count, block_rows, count_of_heads, HD)
    value_blocks = value_all.reshape(block_count, block_rows, count_of_heads, HD)
    total_block_count = numbers.reshape(block_count, block_rows)
    newest_query = jnp.max(query_numbers)

    def advance(running, blocks):
        current_key_block, value_block, key_numbers = blocks

        def unchanged(inside):
            return inside

        def updated(inside):
            return attend_block(
                inside,
                current_key_block,
                value_block,
                key_numbers,
                head_grouped_rows,
                query_numbers,
                score_scale,
            )

        running = lax.cond(jnp.min(key_numbers) > newest_query, unchanged, updated, running)
        return (running, None)

    carried, ignored = lax.scan(advance, carried, (key_blocks, value_blocks, total_block_count))
    return carried


def local(queries, keys, values, router_prob, norm_gain, slot_pos, live_count):
    device_mesh = lax.axis_size("seq")
    my_index = lax.axis_index("seq")
    capacity = queries.shape[0]
    local_heads = queries.shape[1] // HD
    local_groups = keys.shape[1] // HD
    group_size = local_heads // local_groups
    picked_rows = TOK_DEV // 8
    per_peer = (capacity + device_mesh - 1) // device_mesh
    score_scale = 1.0 / math.sqrt(HD)
    counts = lax.all_gather(live_count, "seq", axis=0, tiled=True)
    limits = jnp.cumsum(counts)
    starts = limits - counts
    shard_range = jnp.arange(device_mesh, dtype=jnp.int32)
    self_hot = shard_range == my_index
    start_here = jnp.sum(jnp.where(self_hot, starts, 0))
    count_here = jnp.sum(jnp.where(self_hot, counts, 0))
    slot_index = jnp.arange(capacity, dtype=jnp.int32)
    buffer_range = jnp.arange(device_mesh * per_peer, dtype=jnp.int32)

    def spread(arrays):
        source_slot = (
            jnp.mod(buffer_range // per_peer - start_here, device_mesh)
            + buffer_range % per_peer * device_mesh
        )
        usable = source_slot < count_here
        picker = ((source_slot[:, None] == slot_index[None, :]) & usable[:, None]).astype(
            jnp.bfloat16
        )
        return jnp.dot(picker, arrays, preferred_element_type=jnp.float32).astype(jnp.bfloat16)

    def compact(received, picker):
        return jnp.dot(picker, received, preferred_element_type=jnp.float32).astype(jnp.bfloat16)

    def dense_numbers(positions):
        return positions // picked_rows + positions % picked_rows * device_mesh

    query_numbers = start_here + jnp.minimum(slot_index, count_here - 1)
    row_count = queries.shape[0]
    head_grouped_rows = queries.reshape(row_count, local_groups, group_size, HD)
    initial = (
        jnp.full((local_groups, group_size, row_count), lowest, jnp.float32),
        jnp.zeros((local_groups, group_size, row_count), jnp.float32),
        jnp.zeros((local_groups, group_size, row_count, HD), jnp.float32),
    )
    numbers_here = my_index + jnp.arange(picked_rows, dtype=jnp.int32) * device_mesh
    source = jnp.sum((limits[None, :] <= numbers_here[:, None]).astype(jnp.int32), axis=1)
    source_hot = source[:, None] == shard_range[None, :]
    within = numbers_here - jnp.sum(jnp.where(source_hot, starts[None, :], 0), axis=1)
    row_index = source * per_peer + within // device_mesh
    key_picker = (row_index[:, None] == buffer_range[None, :]).astype(jnp.bfloat16)
    key_in, value_in = in_one_piece((spread(keys), spread(values)), "seq", 0, 0, 1)
    key_dense = compact(key_in, key_picker)
    value_dense = compact(value_in, key_picker)
    key_all, value_all = sent_together((key_dense, value_dense), "seq", 0, 1)
    highest, totals, running_output = fold_blocks(
        initial, key_all, value_all, head_grouped_rows, query_numbers, dense_numbers, score_scale
    )
    attended = (running_output / totals[..., None]).astype(jnp.bfloat16)
    attended = jnp.transpose(attended, (2, 0, 1, 3)).reshape(row_count, local_heads * HD)
    widened = attended.astype(jnp.float32)
    squares = jnp.sum(widened * widened, axis=1)
    total_squares = taken_together(squares, "tp")
    inverse = lax.rsqrt(total_squares / (H * HD) + epsilon)
    normed = (router_prob[:, None] * norm_gain[None, :] * widened * inverse[:, None]).astype(
        jnp.bfloat16
    )
    alive = slot_index < count_here
    placer = (
        (jnp.arange(TOK_DEV, dtype=jnp.int32)[:, None] == slot_pos[None, :]) & alive[None, :]
    ).astype(jnp.bfloat16)
    return jnp.dot(placer, normed, preferred_element_type=jnp.float32).astype(jnp.bfloat16)


def solution(mesh):
    in_specs = (
        P("seq", "tp"),
        P("seq", "tp"),
        P("seq", "tp"),
        P("seq"),
        P("tp"),
        P("seq"),
        P("seq"),
    )
    out_specs = P("seq", "tp")
    return jax.shard_map(local, mesh=mesh, in_specs=in_specs, out_specs=out_specs, check_vma=False)
```

profile of v0, /device:TPU:1, one launch (start us, length us, event | category | flops | bytes accessed | tf_op | source)
XLA Modules:
  0.0 202.2 jit_solution(10926497110232594010)
XLA Ops:
  7.2 1.3 dynamic-slice
  8.5 0.8 dynamic-update-slice
  9.2 27.8 %all-reduce = s32[128]{0:T(128)S(1)} all-reduce(s32[128]{0:T(128)S(1)} %dynamic-update-slice), channel_id=1, replica_groups=mesh['seq'=128,'tp'=4] {'seq'}, use_global_device_ids=true, to_apply=%add | all-reduce | flops 128 | bytes 1024
  37.1 0.2 reduce-window.8
  37.4 0.7 fusion.48
  38.0 0.6 and_select_fusion
  38.6 1.2 broadcast_compare_fusion.1
  39.8 0.2 convolution_convert_fusion.1
  40.1 1.0 convolution_convert_fusion.2
  41.1 0.5 broadcast.293
  41.6 0.7 reduce.5
  42.3 0.7 reshape.165
  43.0 10.9 %all-to-all-start = ((bf16[128,2,256]{2,1,0:T(2,128)(2,1)}), bf16[128,2,256]{2,1,0:T(2,128)(2,1)S(1)}, u32[]{:S(2)}, u32[]{:S(2)}) async-start(bf16[128,2,256]{2,1,0:T(2,128)(2,1)} %reshape.165), calls=%async_computation | async-start | bytes 262144 | tf_op jit(solution)/shard_map/all_to_all | solution.py:22
  54.0 0.2 convert_reduce_fusion
  54.1 0.2 select_reduce_fusion
  54.4 12.3 %all-to-all-done = bf16[128,2,256]{2,1,0:T(2,128)(2,1)S(1)} async-done(((bf16[128,2,256]{2,1,0:T(2,128)(2,1)}), bf16[128,2,256]{2,1,0:T(2,128)(2,1)S(1)}, u32[]{:S(2)}, u32[]{:S(2)}) %all-to-all-start) | async-done | bytes 131104 | tf_op jit(solution)/shard_map/all_to_all | solution.py:22
  66.7 0.2 convolution_convert_fusion.4
  66.9 0.2 convolution_convert_fusion.3
  67.1 0.6 pad_maximum_fusion
  68.4 1.0 reshape.154
  69.5 1.3 add_reduce_fusion
  70.7 0.6 iota_compare_fusion.6
  71.4 73.3 %all-gather.2.cloned.1.call-done = bf16[4096,512]{1,0:T(8,128)(2,1)} async-done(((bf16[32,512]{1,0:T(8,128)(2,1)}), bf16[4096,512]{1,0:T(8,128)(2,1)}) %all-gather.2.cloned.1.call-update) | async-done | bytes 4194320 | tf_op jit(solution)/shard_map/all_gather | solution.py:32
  144.7 3.8 %fusion.52 = (bf16[4096,256]{1,0:T(8,128)(2,1)}, bf16[4096,256]{1,0:T(8,128)(2,1)S(1)}) fusion(bf16[4096,512]{1,0:T(8,128)(2,1)} %all-gather.2.cloned.1.call-done), kind=kLoop, calls=%fused_computation.91 | loop fusion | bytes 8388608 | tf_op jit(solution)/shard_map/split | solution.py:32
  148.5 2.1 %reshape.153 = bf16[4,1024,2,128]{3,2,1,0:T(2,128)(2,1)} reshape(bf16[4096,256]{1,0:T(8,128)(2,1)S(1)} %get-tuple-element.278) | data formatting | bytes 4194304 | tf_op jit(solution)/shard_map/reshape | solution.py:89
  150.6 1.9 copy.36
  152.5 4.0 %reshape.155 = bf16[4,1024,2,128]{3,2,1,0:T(2,128)(2,1)} reshape(bf16[4096,256]{1,0:T(8,128)(2,1)} %get-tuple-element.277) | data formatting | bytes 4194304 | tf_op jit(solution)/shard_map/reshape | solution.py:90
  156.5 3.2 %copy.38 = bf16[4,1024,2,128]{3,1,2,0:T(8,128)(2,1)} copy(bf16[4,1024,2,128]{3,2,1,0:T(2,128)(2,1)} %reshape.155) | data formatting | bytes 4194304
  159.8 25.5 %while.15 = (s32[]{:T(128)}, f32[2,4,96]{2,1,0:T(4,128)S(1)}, f32[2,4,96]{2,1,0:T(4,128)S(1)}, f32[2,4,96,128]{3,2,1,0:T(8,128)S(1)}, s32[4,1024]{1,0:T(4,128)S(...) while((s32[]{:T(128)}, f32[2,4,96]{2,1,0:T(4,128)S(1)}, ...), condition=%wide.region_12.13_spmd.clone, body=%wide.region_6.12_spmd.clone.sunk | while | flops 411601600 | bytes 11925791 | solution.py:114
  159.8 0.6 fusion.57
  161.7 4.4 %conditional.3 = (f32[2,4,96]{2,1,0:T(4,128)S(1)}, f32[2,4,96]{2,1,0:T(4,128)S(1)}, f32[2,4,96,128]{3,2,1,0:T(8,128)S(1)}) conditional(s32[]{:T(128)} %convert_element_type.83, (s32[1,1024]{1,0:T(1,128)S(1)}, s32[]{:T(128)}, bf16[4,1024,2,128]{3,1,2,0:T(8,128)(2,1)S(1)}, s32[]{:T(128)}, bf16[96,2,4,128]{3,0,2,1:T(8,128)(2,1)S(1)}, ...), branch_computations={%region_8.10_spmd, %region_11.11_spmd} | conditional | flops 411600576 | bytes 11910820 | solution.py:111
  161.7 0.6 minimum_add_fusion
  162.3 0.1 broadcast_compare_fusion
  162.4 0.8 fusion.2
  163.2 0.9 fusion.6
  164.2 1.9 fusion.10
  166.2 0.6 fusion.57
  168.1 4.4 %conditional.3 = (f32[2,4,96]{2,1,0:T(4,128)S(1)}, f32[2,4,96]{2,1,0:T(4,128)S(1)}, f32[2,4,96,128]{3,2,1,0:T(8,128)S(1)}) conditional(s32[]{:T(128)} %convert_element_type.83, (s32[1,1024]{1,0:T(1,128)S(1)}, s32[]{:T(128)}, bf16[4,1024,2,128]{3,1,2,0:T(8,128)(2,1)S(1)}, s32[]{:T(128)}, bf16[96,2,4,128]{3,0,2,1:T(8,128)(2,1)S(1)}, ...), branch_computations={%region_8.10_spmd, %region_11.11_spmd} | conditional | flops 411600576 | bytes 11910820 | solution.py:111
  168.1 0.6 minimum_add_fusion
  168.7 0.1 broadcast_compare_fusion
  168.8 0.8 fusion.2
  169.6 0.9 fusion.6
  170.6 1.9 fusion.10
  172.5 0.6 fusion.57
  174.5 4.4 %conditional.3 = (f32[2,4,96]{2,1,0:T(4,128)S(1)}, f32[2,4,96]{2,1,0:T(4,128)S(1)}, f32[2,4,96,128]{3,2,1,0:T(8,128)S(1)}) conditional(s32[]{:T(128)} %convert_element_type.83, (s32[1,1024]{1,0:T(1,128)S(1)}, s32[]{:T(128)}, bf16[4,1024,2,128]{3,1,2,0:T(8,128)(2,1)S(1)}, s32[]{:T(128)}, bf16[96,2,4,128]{3,0,2,1:T(8,128)(2,1)S(1)}, ...), branch_computations={%region_8.10_spmd, %region_11.11_spmd} | conditional | flops 411600576 | bytes 11910820 | solution.py:111
  174.5 0.6 minimum_add_fusion
  175.1 0.1 broadcast_compare_fusion
  175.2 0.8 fusion.2
  176.0 0.9 fusion.6
  176.9 1.9 fusion.10
  178.9 0.6 fusion.57
  180.8 4.4 %conditional.3 = (f32[2,4,96]{2,1,0:T(4,128)S(1)}, f32[2,4,96]{2,1,0:T(4,128)S(1)}, f32[2,4,96,128]{3,2,1,0:T(8,128)S(1)}) conditional(s32[]{:T(128)} %convert_element_type.83, (s32[1,1024]{1,0:T(1,128)S(1)}, s32[]{:T(128)}, bf16[4,1024,2,128]{3,1,2,0:T(8,128)(2,1)S(1)}, s32[]{:T(128)}, bf16[96,2,4,128]{3,0,2,1:T(8,128)(2,1)S(1)}, ...), branch_computations={%region_8.10_spmd, %region_11.11_spmd} | conditional | flops 411600576 | bytes 11910820 | solution.py:111
  180.9 0.6 minimum_add_fusion
  181.4 0.1 broadcast_compare_fusion
  181.6 0.8 fusion.2
  182.4 0.9 fusion.6
  183.3 1.9 fusion.10
  185.3 0.3 fusion.22
  185.5 0.6 broadcast_in_dim.89
  186.1 4.0 %all-to-all-start.1 = ((f32[4,1,96]{2,1,0:T(1,128)}), f32[4,1,96]{2,1,0:T(1,128)S(1)}, u32[]{:S(2)}, u32[]{:S(2)}) async-start(f32[4,1,96]{2,1,0:T(1,128)} %broadcast_in_dim.89), calls=%async_computation.1 | async-start | bytes 4096 | tf_op jit(solution)/shard_map/all_to_all | solution.py:37
  190.1 0.3 copy.39
  190.4 0.2 reshape.156
  190.6 3.6 %all-to-all-done.1 = f32[4,1,96]{2,1,0:T(1,128)S(1)} async-done(((f32[4,1,96]{2,1,0:T(1,128)}), f32[4,1,96]{2,1,0:T(1,128)S(1)}, u32[]{:S(2)}, u32[]{:S(2)}) %all-to-all-start.1) | async-done | bytes 1568 | tf_op jit(solution)/shard_map/all_to_all | solution.py:37
  194.2 1.2 convolution_convert_fusion
  (42 shorter events, 0.7 us)
Async XLA Ops:
  6.5 33.3 %copy-start = (bf16[96,256]{1,0:T(8,128)(2,1)S(1)}, bf16[96,256]{1,0:T(8,128)(2,1)}, u32[]{:S(2)}) copy-start(bf16[96,256]{1,0:T(8,128)(2,1)} %param.13) | copy-start | bytes 147460
  43.0 23.6 %all-to-all-start = ((bf16[128,2,256]{2,1,0:T(2,128)(2,1)}), bf16[128,2,256]{2,1,0:T(2,128)(2,1)S(1)}, u32[]{:S(2)}, u32[]{:S(2)}) async-start(bf16[128,2,256]{2,1,0:T(2,128)(2,1)} %reshape.165), calls=%async_computation | async-start | bytes 262144 | tf_op jit(solution)/shard_map/all_to_all | solution.py:22
  53.9 90.8 %all-gather.2.cloned.1.call-start = ((), (), s32[]{:S(2)}) async-start(), calls=%async_computation.2 | async-start | bytes 4227072 | tf_op jit(solution)/shard_map/all_gather | solution.py:32
  159.7 34.5 %copy-start.1 = (f32[1024]{0:T(1024)S(1)}, f32[1024]{0:T(1024)}, u32[]{:S(2)}) copy-start(f32[1024]{0:T(1024)} %param.15) | copy-start | bytes 12292
  159.7 34.5 %copy-start.2 = (f32[96]{0:T(128)S(1)}, f32[96]{0:T(128)}, u32[]{:S(2)}) copy-start(f32[96]{0:T(128)} %param.14) | copy-start | bytes 1156
  159.7 34.5 %copy-start.3 = (s32[96]{0:T(128)S(1)}, s32[96]{0:T(128)}, u32[]{:S(2)}) copy-start(s32[96]{0:T(128)} %param.16) | copy-start | bytes 1156
  186.1 8.0 %all-to-all-start.1 = ((f32[4,1,96]{2,1,0:T(1,128)}), f32[4,1,96]{2,1,0:T(1,128)S(1)}, u32[]{:S(2)}, u32[]{:S(2)}) async-start(f32[4,1,96]{2,1,0:T(1,128)} %broadcast_in_dim.89), calls=%async_computation.1 | async-start | bytes 4096 | tf_op jit(solution)/shard_map/all_to_all | solution.py:37
Sparse Core Ops, SparseCore 0:
  67.9 76.7 all-gather.1
where the time goes:
time: 203 us; the launch traced here: 202 us
  waiting for transfers between devices  89.2 us (44%)
  blocking collectives  27.8 us (14%)
  local copies, waits for them, and re-layouts  20.6 us (10%)
  other arithmetic  15.9 us (8%)
  starting transfers between devices  14.9 us (7%)
  between operations  14.9 us (7%)
  matrix products  13.6 us (7%)
  loops' own time  5.43 us (3%)
    all_gather x1, waiting for transfers between devices, sent_together(): lax.all_gather(both, axis, axis=dim, tiled=True)  73.3 us
    unnamed x1, blocking collectives  27.8 us
    all_to_all x1, waiting for transfers between devices, in_one_piece(): lax.all_to_all(both, axis, split_axis=split_dim, concat_axis=concat_dim,...  12.3 us
    all_to_all x1, starting transfers between devices, in_one_piece(): lax.all_to_all(both, axis, split_axis=split_dim, concat_axis=concat_dim,...  10.9 us
    unnamed x17, local copies, waits for them, and re-layouts  7.96 us
    dot_general x4, matrix products, attend_block(): jnp.einsum('ycwh,hyu->ycwu', weights.astype(jnp.bfloat16), value_block, p...  7.69 us
    another operation x1, loops' own time, fold_blocks(): lax.scan(advance, carried, (key_blocks, value_blocks, total_block_count))  5.27 us
  transfers between devices with their start and end apart: 3, of which 3 were waited for; matrix products, arithmetic and copies ran while one was open for 2% of the time, Pallas kernels for 0%

commit v1 on v0

v1 whole, which is shorter than its diff:
```python
import math

import jax
import jax.numpy as jnp
from jax import lax
from jax.experimental import pallas as pl
from jax.experimental.pallas import tpu as pltpu
from jax.sharding import PartitionSpec as P

H = 32
HD = 128
TOK_DEV = 256
CAP = 96
SELECTED = 4096
N_SEQ = 128
LOCAL_HEADS = 8
LOCAL_GROUPS = 2
GROUP = 4
KV_COLS = 512
PAYLOAD = CAP + 8
UNIT = 16
BLOCK = 512
TAIL = 640
ROWS = GROUP * CAP
PACKED = SELECTED + N_SEQ * (UNIT - 1)
BUFFER = -(-PACKED // UNIT) * UNIT + TAIL
EPSILON = 1e-06
LOWEST = -1e30
SCALE = math.log2(math.e) / math.sqrt(HD)


def attend_kernel(counts_ref, me_ref, q_ref, kv_ref, out_ref, sq_ref, buf, flags, q_all, m_ref, acc_ref, sem):
    me = me_ref[0]
    flags[...] = jnp.ones_like(flags)

    def bring(s, at):
        n = counts_ref[s]
        size = pl.multiple_of((n + (UNIT - 1)) // UNIT * UNIT, UNIT)
        at = pl.multiple_of(at, UNIT)
        pltpu.make_async_copy(
            kv_ref.at[s, pl.ds(0, size), :], buf.at[pl.ds(at, size), :], sem
        ).start()
        last = pl.multiple_of(at + size - UNIT, UNIT)
        row = lax.broadcasted_iota(jnp.int32, (UNIT, HD), 0)
        alive = jnp.where(row < n - (size - UNIT), 1.0, 0.0)
        flags[pl.ds(last, UNIT), :] = alive.astype(jnp.bfloat16)
        return at + size

    mine = lax.fori_loop(0, me, bring, jnp.int32(0))
    end = pl.multiple_of(bring(me, mine), UNIT)
    for k in range(TAIL // UNIT):
        buf[pl.ds(pl.multiple_of(end + k * UNIT, UNIT), UNIT), :] = jnp.zeros((UNIT, KV_COLS), jnp.bfloat16)
    for g in range(LOCAL_GROUPS):
        for h in range(GROUP):
            at = (g * GROUP + h) * HD
            q_all[g, h * CAP : (h + 1) * CAP, :] = q_ref[:, at : at + HD]
    m_ref[...] = jnp.full_like(m_ref, LOWEST)
    acc_ref[...] = jnp.zeros_like(acc_ref)
    pltpu.make_async_copy(buf.at[pl.ds(0, end), :], buf.at[pl.ds(0, end), :], sem).wait()

    def fold(start, width, masked):
        for g in range(LOCAL_GROUPS):
            keys = buf[pl.ds(start, width), g * HD : (g + 1) * HD]
            values = buf[pl.ds(start, width), (LOCAL_GROUPS + g) * HD : (LOCAL_GROUPS + g + 1) * HD]
            both = jnp.concatenate([values, flags[pl.ds(start, width), :]], axis=1)
            scores = lax.dot_general(
                q_all[g], keys, (((1,), (1,)), ((), ())), preferred_element_type=jnp.float32
            )
            if masked:
                col = lax.broadcasted_iota(jnp.int32, (1, CAP, width), 2)
                row = lax.broadcasted_iota(jnp.int32, (1, CAP, width), 1)
                visible = col - row <= mine - start
                scores = jnp.where(visible, scores.reshape(GROUP, CAP, width), LOWEST)
                scores = scores.reshape(ROWS, width)
            old = m_ref[g]
            new = jnp.maximum(old, jnp.max(scores, axis=1, keepdims=True))
            weights = jnp.exp2((scores - new[:, :1]) * SCALE).astype(jnp.bfloat16)
            factor = jnp.exp2((old - new) * SCALE)
            m_ref[g] = new
            update = jnp.dot(weights, both, preferred_element_type=jnp.float32)
            acc_ref[g] = acc_ref[g] * jnp.concatenate([factor, factor], axis=1) + update

    blocks = mine // BLOCK

    def full(i, _):
        fold(pl.multiple_of(i * BLOCK, BLOCK), BLOCK, False)
        return 0

    lax.fori_loop(0, blocks, full, 0)
    fold(pl.multiple_of(blocks * BLOCK, BLOCK), TAIL, True)
    squares = jnp.zeros((CAP, HD), jnp.float32)
    for g in range(LOCAL_GROUPS):
        acc = acc_ref[g]
        attended = (acc[:, :HD] / acc[:, HD:]).astype(jnp.bfloat16)
        for h in range(GROUP):
            at = (g * GROUP + h) * HD
            piece = attended[h * CAP : (h + 1) * CAP]
            out_ref[:, at : at + HD] = piece
            wide = piece.astype(jnp.float32)
            squares = squares + wide * wide
    square = jnp.concatenate([squares, jnp.zeros((HD - CAP, HD), jnp.float32)], axis=0)
    sq_ref[...] = jnp.sum(jnp.transpose(square), axis=0, keepdims=True)


def attend(counts, me, queries, gathered):
    return pl.pallas_call(
        attend_kernel,
        grid_spec=pltpu.PrefetchScalarGridSpec(
            num_scalar_prefetch=2,
            grid=(),
            in_specs=[
                pl.BlockSpec(memory_space=pltpu.VMEM),
                pl.BlockSpec(memory_space=pl.ANY),
            ],
            out_specs=[
                pl.BlockSpec(memory_space=pltpu.VMEM),
                pl.BlockSpec(memory_space=pltpu.VMEM),
            ],
            scratch_shapes=[
                pltpu.VMEM((BUFFER, KV_COLS), jnp.bfloat16),
                pltpu.VMEM((BUFFER, HD), jnp.bfloat16),
                pltpu.VMEM((LOCAL_GROUPS, ROWS, HD), jnp.bfloat16),
                pltpu.VMEM((LOCAL_GROUPS, ROWS, HD), jnp.float32),
                pltpu.VMEM((LOCAL_GROUPS, ROWS, 2 * HD), jnp.float32),
                pltpu.SemaphoreType.DMA(()),
            ],
        ),
        out_shape=[
            jax.ShapeDtypeStruct((CAP, LOCAL_HEADS * HD), jnp.bfloat16),
            jax.ShapeDtypeStruct((1, HD), jnp.float32),
        ],
        name="attend",
    )(counts, me, queries, gathered)


def local(queries, keys, values, router_prob, norm_gain, slot_pos, live_count):
    slot_index = jnp.arange(CAP, dtype=jnp.int32)
    alive = slot_index < live_count[0]
    sent_keys = jnp.where(alive[:, None], keys, keys[:1])
    sent_values = jnp.where(alive[:, None], values, jnp.zeros_like(values))
    count_rows = jnp.broadcast_to(live_count.astype(jnp.bfloat16)[None, :], (PAYLOAD - CAP, KV_COLS))
    payload = jnp.concatenate([jnp.concatenate([sent_keys, sent_values], axis=1), count_rows], axis=0)
    gathered = lax.all_gather(payload, "seq", axis=0)
    counts = gathered[:, CAP, 0].astype(jnp.int32)
    me = lax.axis_index("seq").astype(jnp.int32).reshape(1)
    attended, squares = attend(counts, me, queries, gathered)
    total_squares = lax.psum(squares, "tp")[0, :CAP]
    inverse = lax.rsqrt(total_squares / (H * HD) + EPSILON)
    widened = attended.astype(jnp.float32)
    normed = (router_prob[:, None] * norm_gain[None, :] * widened * inverse[:, None]).astype(
        jnp.bfloat16
    )
    placer = (
        (jnp.arange(TOK_DEV, dtype=jnp.int32)[:, None] == slot_pos[None, :]) & alive[None, :]
    ).astype(jnp.bfloat16)
    return jnp.dot(placer, normed, preferred_element_type=jnp.float32).astype(jnp.bfloat16)


def solution(mesh):
    in_specs = (
        P("seq", "tp"),
        P("seq", "tp"),
        P("seq", "tp"),
        P("seq"),
        P("tp"),
        P("seq"),
        P("seq"),
    )
    out_specs = P("seq", "tp")
    return jax.shard_map(local, mesh=mesh, in_specs=in_specs, out_specs=out_specs, check_vma=False)
```

time: 203 us -> 142 us (0.70)
  the two profiles are of different devices: /device:TPU:1 before, /device:TPU:472 now
where the time goes in v1:
time: 142 us
  waiting for transfers between devices  91.4 us (64%)
  Pallas kernels  17.7 us (12%)
  between operations  14.1 us (10%)
  blocking collectives  10.4 us (7%)
  other arithmetic  5.39 us (4%)
  matrix products  2.11 us (1%)
    all_gather x1, waiting for transfers between devices, local(): gathered = lax.all_gather(payload, 'seq', axis=0)  91.4 us
    pallas_call x1, Pallas kernels, attend(): pl.pallas_call(attend_kernel, grid_spec=pltpu.PrefetchScalarGridSpec(num_...  17.7 us
    psum x1, blocking collectives, local(): total_squares = lax.psum(squares, 'tp')[0, :CAP]  10.4 us
    convert_element_type x1, other arithmetic, local(): counts = gathered[:, CAP, 0].astype(jnp.int32)  3.82 us
  transfers between devices with their start and end apart: 1, of which 1 were waited for; matrix products, arithmetic and copies ran while one was open for 0% of the time, Pallas kernels for 0%

profile of v1, /device:TPU:472, one launch (start us, length us, event | category | flops | bytes accessed | tf_op | source)
XLA Modules:
  0.0 141.8 jit_solution(2397477440538524103)
XLA Ops:
  6.5 0.0 copy-start.2
  6.5 0.0 copy-start
  6.5 0.0 copy-start.1
  6.5 0.0 all-gather.3.cloned.1.call-start
  7.3 0.7 slice_reduce_fusion
  8.0 0.9 broadcast_select_fusion.1
  8.9 0.7 fusion.7
  9.5 0.0 all-gather.3.cloned.1.call-update
  9.6 91.4 %all-gather.3.cloned.1.call-done = bf16[13312,512]{1,0:T(8,128)(2,1)} async-done(((bf16[104,512]{1,0:T(8,128)(2,1)}), bf16[13312,512]{1,0:T(8,128)(2,1)}) %all-gather.3.cloned.1.call-update) | async-done | bytes 13631504 | tf_op jit(solution)/shard_map/all_gather | solution.py:143
  100.9 3.8 %fusion.8.counts_ref = s32[128]{0:T(128)} fusion(bf16[128,104,512]{2,1,0:T(8,128)(2,1)} %bitcast.7), kind=kLoop, calls=%fused_computation.12 | loop fusion | flops 128 | bytes 768 | tf_op jit(solution)/shard_map/convert_element_type | solution.py:144
  104.8 17.7 %attend.1 = (bf16[96,1024]{1,0:T(8,128)(2,1)}, f32[1,128]{1,0:T(1,128)}) custom-call(s32[128]{0:T(128)} %fusion.8.counts_ref, s32[1]{0:T(128)} %bitcast.3.me_ref, bf16[96,1024]{1,0:T(8,128)(2,1)} %q_ref.1, bf16[128,104,512]{2,1,0:T(8,128)(2,1)} %bitcast.8), custom_call_target="tpu_custom_call" | custom-call | tf_op jit(solution)/shard_map/attend/pallas_call | solution.py:106
  122.4 10.4 %psum.7 = f32[1,128]{1,0:T(1,128)S(1)} all-reduce(f32[1,128]{1,0:T(1,128)} %get-tuple-element.8), channel_id=1, replica_groups=mesh['seq'=128,'tp'=4] {'tp'}, use_global_device_ids=true, to_apply=%region_0.1 | all-reduce | flops 128 | bytes 1024 | tf_op jit(solution)/shard_map/psum | solution.py:147
  132.9 0.0 copy-done.2
  132.9 0.0 copy-done
  132.9 0.0 copy-done.1
  132.9 2.1 %convolution_convert_fusion = bf16[256,1024]{1,0:T(8,128)(2,1)} fusion(bf16[96,1024]{1,0:T(8,128)(2,1)} %get-tuple-element.7, f32[96]{0:T(128)S(1)} %rsqrt_bitcast_fusion, f32[1024]{0:T(1024)S(1)} %copy-done, f32[96]{0:T(128)S(1)} %copy-done.1, s32[96]{0:T(128)S(1)} %copy-done.2, pred[96]{0:T(512)(128)(4,1)S(1)} %iota_compare_fusion.2), kind=kOutput, calls=%fused_computation | convolution fusion | flops 51134464 | bytes 726240 | tf_op jit(solution)/shard_map/dot_general | solution.py:156
  (2 shorter events, 0.0 us)
Async XLA Ops:
  6.5 126.3 %copy-start.2 = (s32[96]{0:T(128)S(1)}, s32[96]{0:T(128)}, u32[]{:S(2)}) copy-start(s32[96]{0:T(128)} %param.12) | copy-start | bytes 1156
  6.5 126.3 %copy-start = (f32[1024]{0:T(1024)S(1)}, f32[1024]{0:T(1024)}, u32[]{:S(2)}) copy-start(f32[1024]{0:T(1024)} %param.11) | copy-start | bytes 12292
  6.5 126.3 %copy-start.1 = (f32[96]{0:T(128)S(1)}, f32[96]{0:T(128)}, u32[]{:S(2)}) copy-start(f32[96]{0:T(128)} %param.10) | copy-start | bytes 1156
  6.5 94.4 %all-gather.3.cloned.1.call-start = ((), (), s32[]{:S(2)}) async-start(), calls=%async_computation | async-start | bytes 13737984 | tf_op jit(solution)/shard_map/all_gather | solution.py:143
Sparse Core Ops, SparseCore 0:
  10.5 90.4 all-gather.2
